TPU v7x, 32 devices: a whole 2x2x4 slice. The times are simulated.
32 devices in a mesh: seq: 8 (over y, x, core), head: 4 (over z).
Axes of the slice: x: 2, y: 2, z: 4, core: 2. Of those that a mesh axis runs over, the one named last changes fastest.
Arguments:
- lat_query: bfloat16 [1024, 73728], P('seq', 'head'), may hold values from -6 to 6
- lat_keys: bfloat16 [1024, 576], P('seq'), may hold values from -6 to 6
- normalizer: float32 [1024, 128], P('seq'), may hold values from 3 to 7
- lookback: int32 [1024], P('seq'), may hold values from 1 to 1024
- index_query: bfloat16 [1024, 8192], P(('seq', 'head')), may hold values from -20 to 20
- index_keys: bfloat16 [1024, 128], P('seq'), may hold values from -6 to 6
- index_weight: float32 [1024, 64], P(('seq', 'head')), may hold values from 0.25 to 2
Outputs:
- grad_query: float32 [1024, 8192], P(('seq', 'head'))
- grad_weight: float32 [1024, 64], P(('seq', 'head'))
- grad_key: float32 [1024, 128], P(('seq', 'head'))
All inputs are finite; a program needn't handle non-finite values.
Results may differ from a plain program's by a relative error of at most 0.0029.
Values may be sent and summed in bfloat16 or wider, within the bound.
No kernel may reach another device: no remote copies, remote signals or barrier semaphores. Data moves between devices by JAX's collectives and lax.ppermute only.
A program may use at most 64 MiB of HBM per device.

v0:
```python
import math

import jax
import jax.numpy as jnp
from jax import lax
from jax.sharding import PartitionSpec as P

KDIM = 576


def index_pass(query, weight, target, key_rows, row_pos, row_low):
    row_count = query.shape[0]
    head_count = weight.shape[1]
    key_depth = key_rows.shape[1]
    seq_total = key_rows.shape[0]
    block_rows = min(512, seq_total)
    blocks = seq_total // block_rows
    flat_query = query.reshape(row_count * head_count, key_depth)
    flat_weight = weight.reshape(row_count * head_count)
    factor = key_depth ** (-0.5)

    def scores(block_index):
        key_part = lax.dynamic_slice_in_dim(key_rows, block_index * block_rows, block_rows, 0)
        inner = (
            lax.dot_general(
                flat_query, key_part, (((1,), (1,)), ((), ())), preferred_element_type=jnp.float32
            )
            * factor
        )
        active = jnp.maximum(inner, 0.0)
        summed = jnp.sum(
            (active * flat_weight[:, None]).reshape(row_count, head_count, block_rows), axis=1
        )
        key_pos = block_index * block_rows + jnp.arange(block_rows, dtype=jnp.int32)
        visible = (key_pos[None, :] <= row_pos[:, None]) & (key_pos[None, :] >= row_low[:, None])
        return (key_part, inner, active, summed, visible)

    def first_pass(running, block_index):
        row_top, row_mass = running
        _, _, _, summed, visible = scores(block_index)
        summed = jnp.where(visible, summed, -jnp.inf)
        new_top = jnp.maximum(row_top, jnp.max(summed, axis=1))
        row_mass = row_mass * jnp.exp(row_top - new_top) + jnp.sum(
            jnp.exp(summed - new_top[:, None]), axis=1
        )
        return ((new_top, row_mass), None)

    start_state = (jnp.full((row_count,), -1e30, jnp.float32), jnp.zeros((row_count,), jnp.float32))
    (row_top, row_mass), _ = lax.scan(first_pass, start_state, jnp.arange(blocks, dtype=jnp.int32))

    def second_pass(running, block_index):
        d_query, d_weight = running
        key_part, inner, active, summed, visible = scores(block_index)
        predicted = jnp.where(visible, jnp.exp(summed - row_top[:, None]) / row_mass[:, None], 0.0)
        target_block = lax.dynamic_slice_in_dim(target, block_index * block_rows, block_rows, 1)
        gap_term = predicted - target_block
        d_weight = d_weight + jnp.sum(
            active.reshape(row_count, head_count, block_rows) * gap_term[:, None, :], axis=2
        )
        spread = (gap_term[:, None, :] * weight[:, :, None]).reshape(
            row_count * head_count, block_rows
        ) * factor
        slopes = jnp.where(inner > 0, spread, 0.0).astype(jnp.bfloat16)
        d_query = d_query + jnp.dot(slopes, key_part, preferred_element_type=jnp.float32)
        d_key = lax.dot_general(
            slopes, flat_query, (((0,), (0,)), ((), ())), preferred_element_type=jnp.float32
        )
        return ((d_query, d_weight), d_key)

    start_grads = (
        jnp.zeros((row_count * head_count, key_depth), jnp.float32),
        jnp.zeros((row_count, head_count), jnp.float32),
    )
    (d_query, d_weight), d_key = lax.scan(
        second_pass, start_grads, jnp.arange(blocks, dtype=jnp.int32)
    )
    return (
        d_query.reshape(row_count, head_count * key_depth),
        d_weight,
        d_key.reshape(seq_total, key_depth),
    )


def per_device(lat_query, lat_keys, normalizer, lookback, index_query, index_keys, index_weight):
    local_rows = lat_query.shape[0]
    seq_count = lax.axis_size("seq")
    seq_total = local_rows * seq_count
    first_row = lax.axis_index("seq") * local_rows
    index_rows = index_query.shape[0]
    head_offset = lax.axis_index("head") * index_rows
    score_scale = KDIM ** (-0.5)
    head_count = lat_query.shape[1] // KDIM
    flat_query = lat_query.reshape(local_rows * head_count, KDIM)
    offsets = lax.dynamic_slice_in_dim(
        normalizer, lax.axis_index("head") * head_count, head_count, 1
    )
    query_pos = first_row + jnp.arange(local_rows, dtype=jnp.int32)
    query_low = query_pos - lookback
    lowest = jnp.min(query_low)
    highest = jnp.max(query_pos)
    start = jnp.int32(0)
    mass_rows = jnp.zeros((local_rows, seq_total), jnp.float32)
    latent = lax.all_gather(lat_keys, "seq", axis=0, tiled=True)
    indexed = lax.all_gather(index_keys, "seq", axis=0, tiled=True)
    piece_rows = latent.shape[0]
    key_store = indexed
    sub_rows = math.gcd(piece_rows, 512)

    def sweep(summed):

        def step(sub_index, current):
            begin = sub_index * sub_rows
            key_part = lax.dynamic_slice_in_dim(latent, sub_index * sub_rows, sub_rows, 0)
            scores = lax.dot_general(
                flat_query, key_part, (((1,), (1,)), ((), ())), preferred_element_type=jnp.float32
            )
            expo = jnp.exp(
                scores.reshape(local_rows, head_count, sub_rows) * score_scale - offsets[:, :, None]
            )
            key_pos = begin + jnp.arange(sub_rows, dtype=jnp.int32)
            visible = (key_pos[None, :] <= query_pos[:, None]) & (
                key_pos[None, :] >= query_low[:, None]
            )
            contrib = jnp.where(visible, jnp.sum(expo, axis=1), 0.0)
            return lax.dynamic_update_slice(current, contrib, (jnp.int32(0), begin))

        return lax.fori_loop(0, piece_rows // sub_rows, step, summed)

    skipped = (start > highest) | (start + piece_rows - 1 < lowest)
    mass_rows = lax.cond(skipped, lambda unchanged: unchanged, sweep, mass_rows)
    mass_rows, key_store = (mass_rows, key_store)
    shares = lax.psum_scatter(mass_rows, "head", scatter_dimension=0, tiled=True)
    target = shares / jnp.sum(shares, axis=1, keepdims=True)
    row_pos = first_row + head_offset + jnp.arange(index_rows, dtype=jnp.int32)
    row_low = row_pos - lax.dynamic_slice_in_dim(lookback, head_offset, index_rows, 0)
    grad_query, grad_weight, key_terms = index_pass(
        index_query, index_weight, target, key_store, row_pos, row_low
    )
    grad_key = lax.psum_scatter(key_terms, ("seq", "head"), scatter_dimension=0, tiled=True)
    return (grad_query, grad_weight, grad_key)


def solution(mesh):
    return jax.shard_map(
        per_device,
        mesh=mesh,
        in_specs=(
            P("seq", "head"),
            P("seq", None),
            P("seq", None),
            P("seq"),
            P(("seq", "head"), None),
            P("seq", None),
            P(("seq", "head"), None),
        ),
        out_specs=(P(("seq", "head"), None), P(("seq", "head"), None), P(("seq", "head"), None)),
        check_vma=False,
    )
```

profile of v0, /device:TPU:0, one launch (start us, length us, event | category | flops | bytes accessed | tf_op | source)
XLA Modules:
  0.0 333.1 jit_solution(6634502671684856582)
XLA Ops:
  7.2 1.7 copy.25
  9.0 0.6 fusion.20
  10.3 1.3 fusion.21
  12.2 1.3 reshape.71
  13.5 0.8 mul.140
  14.3 11.5 %all_gather.6 = bf16[1024,128]{1,0:T(8,128)(2,1)S(1)} all-gather(bf16[128,128]{1,0:T(8,128)(2,1)} %param.20), channel_id=1, replica_groups=mesh['seq'=8,'head'=4] {'seq'}, dimensions={0}, use_global_device_ids=true | all-gather | bytes 294912 | tf_op jit(solution)/shard_map/all_gather | solution.py:104
  25.8 1.3 dynamic-slice_subtract_fusion.1
  27.1 10.9 %all-gather.2.cloned.1.call-done = bf16[1024,576]{1,0:T(8,128)(2,1)} async-done(((bf16[128,576]{1,0:T(8,128)(2,1)}), bf16[1024,576]{1,0:T(8,128)(2,1)}) %all-gather.2.cloned.1.call-update) | async-done | bytes 1179664 | tf_op jit(solution)/shard_map/all_gather | solution.py:103
  38.0 53.3 %conditional.1 = (f32[128,1024]{1,0:T(8,128)S(1)}) conditional(s32[]{:T(128)} %convert_element_type.6, (bf16[128,18432]{1,0:T(8,128)(2,1)}, f32[128,128]{1,0:T(8,128)}, s32[]{:T(128)}, s32[128]{0:T(128)S(1)}, s32[128]{0:T(128)S(1)}, /*index=5*/bf16[1024,576]{1,0:T(8,128)(2,1)}) %tuple.40, () %tuple.41), branch_computations={%region_7.11_spmd, %region_11.12_spmd} | conditional | flops 2422407680 | bytes 54711632 | solution.py:130
  38.0 9.9 %reshape.66 = bf16[4096,576]{1,0:T(8,128)(2,1)} reshape(bf16[128,18432]{1,0:T(8,128)(2,1)} %get-tuple-element.287) | data formatting | bytes 9437184 | tf_op jit(solution)/shard_map/reshape | solution.py:93
  48.1 43.2 %while.44 = (s32[]{:T(128)}, f32[128,1024]{1,0:T(8,128)S(1)}, s32[128]{0:T(128)S(1)}, s32[128]{0:T(128)S(1)}, bf16[1024,576]{1,0:T(8,128)(2,1)S(1)}, /*index=5*/...) while((s32[]{:T(128)}, f32[128,1024]{1,0:T(8,128)S(1)}, ...), condition=%wide.region_10.10_spmd, body=%wide.region_8.9_spmd.sunk | while | flops 2422407680 | bytes 39736488 | solution.py:127
  48.1 8.1 %multiply_bitcast_fusion.6 = f32[4096,512]{0,1:T(8,128)} fusion(bf16[4096,576]{1,0:T(8,128)(2,1)} %get-tuple-element.748, bf16[1024,576]{1,0:T(8,128)(2,1)S(1)} %get-tuple-element.747, s32[]{:T(128)S(6)} %select_n.70), kind=kOutput, calls=%fused_computation.3.clone.1 | convolution fusion | flops 2418016256 | bytes 13762564 | tf_op jit(solution)/shard_map/cond/branch_0_fun/while/body/eval_jaxpr/dot_general | solution.py:114
  56.3 9.0 %copy.36 = f32[4096,512]{1,0:T(8,128)} copy(f32[4096,512]{0,1:T(8,128)} %multiply_bitcast_fusion.6) | data formatting | bytes 16777216 | tf_op jit(solution)/shard_map/cond/branch_0_fun/while/body/eval_jaxpr/mul | solution.py:118
  65.3 4.3 %exponential_reduce_fusion.6 = f32[128,512]{1,0:T(8,128)S(1)} fusion(f32[128,32]{1,0:T(8,128)S(1)} %get-tuple-element.749, f32[4096,512]{1,0:T(8,128)} %copy.36), kind=kLoop, calls=%fused_computation.2.clone.1 | loop fusion | flops 4128768 | bytes 8667136 | tf_op jit(solution)/shard_map/cond/branch_0_fun/while/body/eval_jaxpr/reduce_sum | solution.py:124
  69.7 8.2 %multiply_bitcast_fusion.6 = f32[4096,512]{0,1:T(8,128)} fusion(bf16[4096,576]{1,0:T(8,128)(2,1)} %get-tuple-element.748, bf16[1024,576]{1,0:T(8,128)(2,1)S(1)} %get-tuple-element.747, s32[]{:T(128)S(6)} %select_n.70), kind=kOutput, calls=%fused_computation.3.clone.1 | convolution fusion | flops 2418016256 | bytes 13762564 | tf_op jit(solution)/shard_map/cond/branch_0_fun/while/body/eval_jaxpr/dot_general | solution.py:114
  77.9 9.0 %copy.36 = f32[4096,512]{1,0:T(8,128)} copy(f32[4096,512]{0,1:T(8,128)} %multiply_bitcast_fusion.6) | data formatting | bytes 16777216 | tf_op jit(solution)/shard_map/cond/branch_0_fun/while/body/eval_jaxpr/mul | solution.py:118
  86.9 4.3 %exponential_reduce_fusion.6 = f32[128,512]{1,0:T(8,128)S(1)} fusion(f32[128,32]{1,0:T(8,128)S(1)} %get-tuple-element.749, f32[4096,512]{1,0:T(8,128)} %copy.36), kind=kLoop, calls=%fused_computation.2.clone.1 | loop fusion | flops 4128768 | bytes 8667136 | tf_op jit(solution)/shard_map/cond/branch_0_fun/while/body/eval_jaxpr/reduce_sum | solution.py:124
  91.4 0.8 copy-done
  92.4 30.8 %while.45 = (s32[]{:T(128)}, f32[32]{0:T(128)}, f32[32]{0:T(128)}, s32[2]{0:T(128)S(1)}, s32[32]{0:T(128)}, /*index=5*/bf16[1024,128]{1,0:T(8,128)(2,1)S(1)}, bf...) while((s32[]{:T(128)}, f32[32]{0:T(128)}, f32[32]{0:T(128)}, ...), condition=%wide.wide.region_4.5_spmd.clone, body=%wide.wide.region_0.4_spmd.clone.sunk | while | flops 272794304 | bytes 17646036 | solution.py:49
  92.4 0.6 dynamic_slice.65
  93.7 2.6 multiply_bitcast_fusion.5
  96.3 5.4 %copy.33 = f32[2048,512]{1,0:T(8,128)} copy(f32[2048,512]{0,1:T(8,128)} %multiply_bitcast_fusion.5) | data formatting | bytes 8388608 | tf_op jit(solution)/shard_map/while/body/eval_jaxpr/mul | solution.py:32
  101.7 2.8 bitcast_reduce_fusion.6
  104.5 0.8 fusion.57
  105.3 0.8 exponential_reduce_fusion.5
  106.7 0.5 copy.52
  107.2 0.6 dynamic_slice.65
  108.4 2.6 multiply_bitcast_fusion.5
  111.1 5.4 %copy.33 = f32[2048,512]{1,0:T(8,128)} copy(f32[2048,512]{0,1:T(8,128)} %multiply_bitcast_fusion.5) | data formatting | bytes 8388608 | tf_op jit(solution)/shard_map/while/body/eval_jaxpr/mul | solution.py:32
  116.4 2.8 bitcast_reduce_fusion.6
  119.2 0.8 fusion.57
  120.1 0.6 fusion.58
  120.7 0.8 exponential_reduce_fusion.5
  121.5 1.1 fusion.59
  122.6 0.5 copy.52
  123.2 0.8 mul.147
  124.0 1.0 reduce_sum.60
  125.0 1.0 broadcast_divide_fusion
  126.5 62.8 %while.46 = (s32[]{:T(128)}, f32[2048,128]{1,0:T(8,128)}, f32[32,64]{1,0:T(8,128)}, f32[2,512,128]{2,1,0:T(8,128)S(1)}, s32[2]{0:T(128)}, /*index=5*/bf16[1024,1...) while((s32[]{:T(128)}, f32[2048,128]{1,0:T(8,128)}, ...), condition=%wide.wide.region_17.18_spmd.clone, body=%wide.wide.region_14.17_spmd.clone.sunk | while | flops 819563008 | bytes 52302720 | solution.py:74
  126.5 1.2 dynamic_slice.69
  128.3 3.9 %bitcast_multiply_fusion.4 = (f32[2048,512]{0,1:T(8,128)}, f32[512,2048]{1,0:T(8,128)}) fusion(f32[2048]{0:T(1024)S(1)} %get-tuple-element.845, bf16[2048,128]{1,0:T(8,128)(2,1)S(1)} %get-tuple-element.838, bf16[1024,128]{1,0:T(8,128)(2,1)S(1)} %get-tuple-element.837, s32[]{:T(128)S(6)} %select_n.68), kind=kOutput, calls=%fused_computation.25.clone.clone.1 | convolution fusion | flops 271581184 | bytes 9052164 | tf_op jit(solution)/shard_map/while/body/eval_jaxpr/dot_general | solution.py:25
  132.3 5.3 %copy.34 = f32[2048,512]{1,0:T(8,128)} copy(f32[2048,512]{0,1:T(8,128)} %get-tuple-element.710) | data formatting | bytes 8388608 | tf_op jit(solution)/shard_map/while/body/eval_jaxpr/mul | solution.py:32
  137.6 2.8 bitcast_reduce_fusion.7
  140.4 0.7 dynamic-slice_subtract_fusion.4
  141.2 2.5 mul.181
  143.7 5.4 %copy.35 = f32[2048,512]{0,1:T(8,128)} copy(f32[2048,512]{1,0:T(8,128)} %bitcast.79) | data formatting | bytes 8388608 | tf_op jit(solution)/shard_map/while/body/eval_jaxpr/mul | solution.py:60
  149.1 4.7 %fusion.65 = (f32[2048]{0:T(1024)S(1)}, bf16[2048,512]{0,1:T(8,128)(2,1)S(1)}) fusion(f32[2048,512]{0,1:T(8,128)} %copy.35, f32[512,2048]{1,0:T(8,128)} %get-tuple-element.711, f32[2048]{0:T(1024)S(1)} %get-tuple-element.845), kind=kLoop, calls=%fused_computation.26.clone.clone.1 | loop fusion | flops 9435136 | bytes 10502144 | tf_op jit(solution)/shard_map/while/body/eval_jaxpr/reduce_sum | solution.py:57
  153.7 1.8 convolution_add_fusion.3
  155.6 0.7 fusion.66
  156.3 0.6 select_add_fusion.3
  156.9 1.2 dynamic_slice.69
  158.8 3.9 %bitcast_multiply_fusion.4 = (f32[2048,512]{0,1:T(8,128)}, f32[512,2048]{1,0:T(8,128)}) fusion(f32[2048]{0:T(1024)S(1)} %get-tuple-element.845, bf16[2048,128]{1,0:T(8,128)(2,1)S(1)} %get-tuple-element.838, bf16[1024,128]{1,0:T(8,128)(2,1)S(1)} %get-tuple-element.837, s32[]{:T(128)S(6)} %select_n.68), kind=kOutput, calls=%fused_computation.25.clone.clone.1 | convolution fusion | flops 271581184 | bytes 9052164 | tf_op jit(solution)/shard_map/while/body/eval_jaxpr/dot_general | solution.py:25
  162.7 5.3 %copy.34 = f32[2048,512]{1,0:T(8,128)} copy(f32[2048,512]{0,1:T(8,128)} %get-tuple-element.710) | data formatting | bytes 8388608 | tf_op jit(solution)/shard_map/while/body/eval_jaxpr/mul | solution.py:32
  168.1 2.8 bitcast_reduce_fusion.7
  170.9 0.7 dynamic-slice_subtract_fusion.4
  171.6 2.5 mul.181
  174.1 5.4 %copy.35 = f32[2048,512]{0,1:T(8,128)} copy(f32[2048,512]{1,0:T(8,128)} %bitcast.79) | data formatting | bytes 8388608 | tf_op jit(solution)/shard_map/while/body/eval_jaxpr/mul | solution.py:60
  179.5 4.7 %fusion.65 = (f32[2048]{0:T(1024)S(1)}, bf16[2048,512]{0,1:T(8,128)(2,1)S(1)}) fusion(f32[2048,512]{0,1:T(8,128)} %copy.35, f32[512,2048]{1,0:T(8,128)} %get-tuple-element.711, f32[2048]{0:T(1024)S(1)} %get-tuple-element.845), kind=kLoop, calls=%fused_computation.26.clone.clone.1 | loop fusion | flops 9435136 | bytes 10502144 | tf_op jit(solution)/shard_map/while/body/eval_jaxpr/reduce_sum | solution.py:57
  184.2 3.0 convolution_add_fusion.3
  187.2 0.7 fusion.66
  188.0 1.3 select_add_fusion.3
  189.3 0.8 copy-done.1
  190.1 2.4 reshape.72
  192.5 134.0 %reduce-scatter.5.cloned.1.call-done = f32[32,128]{1,0:T(8,128)} async-done(((f32[1024,128]{1,0:T(8,128)}), f32[32,128]{1,0:T(8,128)}) %reduce-scatter.5.cloned.1.call-update) | async-done | bytes 16400 | tf_op jit(solution)/shard_map/reduce_scatter | solution.py:139
  (38 shorter events, 1.9 us)
Async XLA Ops:
  7.2 30.8 %all-gather.2.cloned.1.call-start = ((), (), s32[]{:S(2)}) async-start(), calls=%async_computation.2 | async-start | bytes 1474560 | tf_op jit(solution)/shard_map/all_gather | solution.py:103
  8.9 115.0 %reduce-scatter.3.cloned.1.call-start = ((), (), s32[]{:S(2)}) async-start(), calls=%async_computation.3 | async-start | bytes 655360 | tf_op jit(solution)/shard_map/reduce_scatter | solution.py:132
  38.0 10.0 %copy-start.2 = (f32[128,128]{1,0:T(8,128)S(1)}, f32[128,128]{1,0:T(8,128)}, u32[]{:S(2)}) copy-start(f32[128,128]{1,0:T(8,128)} %get-tuple-element.288) | copy-start | bytes 196612 | tf_op jit(solution)/shard_map/cond
  38.0 10.1 %copy-start.3 = (bf16[1024,576]{1,0:T(8,128)(2,1)S(1)}, bf16[1024,576]{1,0:T(8,128)(2,1)}, u32[]{:S(2)}) copy-start(bf16[1024,576]{1,0:T(8,128)(2,1)} %get-tuple-element.725) | copy-start | bytes 3538948 | tf_op jit(solution)/shard_map/cond
  91.4 0.8 copy-start
  92.2 234.4 %reduce-scatter.5.cloned.1.call-start = ((), (), s32[]{:S(2)}) async-start(), calls=%async_computation.4 | async-start | bytes 540672 | tf_op jit(solution)/shard_map/reduce_scatter | solution.py:139
  189.3 0.8 copy-start.1
Sparse Core Ops, SparseCore 0:
  10.4 27.5 all-gather.1
  92.3 21.8 reduce-scatter.2
  190.3 136.2 reduce-scatter.4
where the time goes:
time: 335 us; the launch traced here: 333 us
  waiting for transfers between devices  145 us (43%)
  local copies, waits for them, and re-layouts  79.2 us (24%)
  other arithmetic  43.5 us (13%)
  matrix products  35.7 us (11%)
  between operations  15.1 us (5%)
  blocking collectives  11.5 us (3%)
    reduce_scatter x1, waiting for transfers between devices, per_device(): lax.psum_scatter(key_terms, ('seq', 'head'), scatter_dimension=0, tiled=T...  134 us
    mul x6, local copies, waits for them, and re-layouts, scores(): active * flat_weight[:, None]  23 us
    mul x2, local copies, waits for them, and re-layouts, step(): scores.reshape(local_rows, head_count, sub_rows) * score_scale  18 us
    dot_general x2, matrix products, step(): lax.dot_general(flat_query, key_part, (((1,), (1,)), ((), ())), preferred...  16.3 us
    mul x4, local copies, waits for them, and re-layouts, second_pass(): gap_term[:, None, :] * weight[:, :, None]  15.8 us
    dot_general x4, matrix products, scores(): lax.dot_general(flat_query, key_part, (((1,), (1,)), ((), ())), preferred...  13.2 us
    all_gather x1, blocking collectives, per_device(): indexed = lax.all_gather(index_keys, 'seq', axis=0, tiled=True)  11.5 us
    reduce_sum x4, other arithmetic, scores(): jnp.sum((active * flat_weight[:, None]).reshape(row_count, head_count, bl...  11.2 us
  transfers between devices with their start and end apart: 3, of which 2 were waited for; matrix products, arithmetic and copies ran while one was open for 11% of the time, Pallas kernels for 0%

commit v1 on v0

v1 whole, which is shorter than its diff:
```python
import functools
import math

import jax
import jax.numpy as jnp
from jax import lax
from jax.experimental import pallas as pl
from jax.experimental.pallas import tpu as pltpu
from jax.sharding import PartitionSpec as P

KDIM = 576
LANES = 128
LOG2E = 1.0 / math.log(2.0)


def shape_of(dims, kind):
    return jax.ShapeDtypeStruct(dims, kind)


def full_spec(dims):
    return pl.BlockSpec(dims, lambda *_: (0,) * len(dims))


def spread_kernel(first, rows, norm_ref, weight_ref, look_ref, off_ref, scale_ref, low_ref, tall):
    heads, local_rows, _ = off_ref.shape
    turn = lax.axis_index("head") * heads
    offsets = norm_ref[...] * LOG2E
    width = offsets.shape[1]
    offsets = pltpu.roll(offsets, lax.rem(width - turn, width), 1)
    for head in range(heads):
        off_ref[head] = jnp.broadcast_to(offsets[:, head : head + 1], (local_rows, LANES))
    weights = weight_ref[...] * first
    for head in range(scale_ref.shape[0]):
        scale_ref[head] = jnp.broadcast_to(weights[:, head : head + 1], (rows, LANES))
    look = jnp.broadcast_to(look_ref[...].astype(jnp.float32), (LANES, look_ref.shape[1]))
    tall[...] = jnp.transpose(look)
    low_ref[...] = tall[pl.ds(lax.axis_index("head") * rows, rows), :]


def spread(normalizer, weight, lookback, heads, factor):
    rows, index_heads = weight.shape
    local_rows = normalizer.shape[0]
    out = (
        shape_of((heads, local_rows, LANES), jnp.float32),
        shape_of((index_heads, rows, LANES), jnp.float32),
        shape_of((rows, LANES), jnp.float32),
    )
    return pl.pallas_call(
        functools.partial(spread_kernel, factor, rows),
        out_shape=out,
        scratch_shapes=[pltpu.VMEM((local_rows, LANES), jnp.float32)],
        compiler_params=pltpu.CompilerParams(vmem_limit_bytes=16 << 20),
        cost_estimate=pl.CostEstimate(flops=4_000_000, bytes_accessed=0, transcendentals=0),
        name="spread",
    )(normalizer, weight, lookback.reshape(1, local_rows))


def mass_kernel(slots, group, query_ref, off_ref, *refs):
    blocks = refs[:slots]
    outs = refs[slots:-2]
    keys, acc = refs[-2:]
    step = pl.program_id(0)
    steps = pl.num_programs(0)
    pad = LANES - KDIM % LANES
    depth = KDIM + pad
    tiles, local_rows, wide = acc.shape
    per_tile = wide // LANES

    @pl.when(step == 0)
    def _():
        acc[...] = jnp.zeros_like(acc)
        for tile in range(tiles):
            keys[tile, :pad] = jnp.zeros((pad, wide), keys.dtype)
            keys[tile, pad + KDIM :] = jnp.zeros((pad, wide), keys.dtype)
            for part in range(per_tile):
                keys[tile, pad : pad + KDIM, part * LANES : (part + 1) * LANES] = blocks[
                    tile * per_tile + part
                ][:KDIM]

    scale = KDIM ** (-0.5) * LOG2E

    @pl.loop(0, tiles)
    def _(tile):
        total = acc[tile]
        for odd in range(2):
            begin = 0 if odd else pad
            picked = [
                query_ref[:, head * KDIM - (pad if odd else 0) : head * KDIM - (pad if odd else 0) + depth]
                for head in range(odd, group, 2)
            ]
            scores = jnp.dot(
                jnp.concatenate(picked, axis=0),
                keys[tile, begin : begin + depth],
                preferred_element_type=jnp.float32,
            )
            for place, head in enumerate(range(odd, group, 2)):
                offset = off_ref[head]
                part = scores[place * local_rows : (place + 1) * local_rows]
                total = total + jnp.exp2(part * scale - jnp.concatenate([offset] * per_tile, axis=1))
        acc[tile] = total

    @pl.when(step == steps - 1)
    def _():
        own, sends = outs[0], outs[1:]
        rows = own.shape[0]
        size = len(sends) + 1
        me = lax.axis_index("head")
        for tile in range(tiles):
            lanes = slice(tile * wide, (tile + 1) * wide)
            own[:, lanes] = acc[tile, pl.ds(me * rows, rows), :]
            for hop, send in enumerate(sends):
                there = lax.rem(me + hop + 1, size)
                send[:, lanes] = acc[tile, pl.ds(there * rows, rows), :].astype(send.dtype)


def attention_mass(lat_query, offsets, blocks, rows, peers):
    local_rows = lat_query.shape[0]
    heads = offsets.shape[0]
    group = min(8, heads)
    slots = len(blocks)
    wide = 2 * LANES
    tiles = slots * LANES // wide
    pad = LANES - KDIM % LANES
    part = shape_of((rows, slots * LANES), jnp.bfloat16)
    outs = (shape_of(part.shape, jnp.float32),) + (part,) * (peers - 1)
    return pl.pallas_call(
        functools.partial(mass_kernel, slots, group),
        out_shape=outs,
        grid=(heads // group,),
        in_specs=[
            pl.BlockSpec((local_rows, group * KDIM), lambda step: (0, step)),
            pl.BlockSpec((group, local_rows, LANES), lambda step: (step, 0, 0)),
        ]
        + [full_spec(block.shape) for block in blocks],
        out_specs=[full_spec(out.shape) for out in outs],
        scratch_shapes=[
            pltpu.VMEM((tiles, KDIM + 2 * pad, wide), jnp.bfloat16),
            pltpu.VMEM((tiles, local_rows, wide), jnp.float32),
        ],
        compiler_params=pltpu.CompilerParams(vmem_limit_bytes=20 << 20),
        cost_estimate=pl.CostEstimate(
            flops=2 * local_rows * heads * KDIM * slots * LANES, bytes_accessed=0, transcendentals=0
        ),
        name="mass",
    )(lat_query, offsets, *blocks)


def stack_heads(value, heads, dims):
    parts = [value[:, head * dims : (head + 1) * dims] for head in range(heads)]
    if value.shape[0] % 16 == 0:
        return jnp.concatenate(parts, axis=0)
    parts = [part.astype(jnp.float32) for part in parts]
    return jnp.concatenate(parts, axis=0).astype(value.dtype)


def score_kernel(slots, query_ref, scale_ref, low_ref, *refs):
    blocks = refs[:slots]
    active_ref, predicted_ref, keys, score = refs[slots:]
    step = pl.program_id(0)
    heads, rows, seq_total = active_ref.shape
    dims = keys.shape[1]

    @pl.when(step == 0)
    def _():
        score[...] = jnp.zeros_like(score)
        for slot in range(slots):
            keys[slot * LANES : (slot + 1) * LANES] = blocks[slot][KDIM:]

    stacked = stack_heads(query_ref[...], heads, dims)
    wide = 2 * LANES
    for begin in range(0, seq_total, wide):
        inner = lax.dot_general(
            stacked,
            keys[begin : begin + wide],
            (((1,), (1,)), ((), ())),
            preferred_element_type=jnp.float32,
        )
        total = score[:, begin : begin + wide]
        for head in range(heads):
            active = jnp.maximum(inner[head * rows : (head + 1) * rows], 0.0)
            active_ref[head, :, begin : begin + wide] = active
            total = total + active * jnp.concatenate([scale_ref[head]] * 2, axis=1)
        score[:, begin : begin + wide] = total

    @pl.when(step == pl.num_programs(0) - 1)
    def _():
        seq = lax.axis_index("seq")
        query_pos = (
            (seq * lax.axis_size("head") + lax.axis_index("head")) * rows
            + lax.broadcasted_iota(jnp.int32, (rows, LANES), 0)
        )
        low = query_pos - low_ref[...].astype(jnp.int32)
        lane = lax.broadcasted_iota(jnp.int32, (rows, LANES), 1)
        seen = []
        for slot in range(slots):
            key_pos = jnp.bitwise_xor(seq, slot) * LANES + lane
            seen.append((key_pos <= query_pos) & (key_pos >= low))
        parts = [score[:, slot * LANES : (slot + 1) * LANES] for slot in range(slots)]
        parts = [jnp.where(see, part, -jnp.inf) for see, part in zip(seen, parts)]
        top = functools.reduce(jnp.maximum, parts)
        top = jnp.max(top, axis=1, keepdims=True)
        parts = [jnp.exp(part - top) for part in parts]
        mass = jnp.sum(functools.reduce(jnp.add, parts), axis=1, keepdims=True)
        for slot in range(slots):
            predicted_ref[:, slot * LANES : (slot + 1) * LANES] = jnp.where(
                seen[slot], parts[slot] / mass, -1.0
            )


def index_scores(index_query, scales, lows, blocks, dims):
    rows = index_query.shape[0]
    index_heads = scales.shape[0]
    group = min(8, index_heads)
    slots = len(blocks)
    seq_total = slots * LANES
    return pl.pallas_call(
        functools.partial(score_kernel, slots),
        out_shape=(
            shape_of((index_heads, rows, seq_total), jnp.float32),
            shape_of((rows, seq_total), jnp.float32),
            shape_of((seq_total, dims), jnp.bfloat16),
        ),
        grid=(index_heads // group,),
        in_specs=[
            pl.BlockSpec((rows, group * dims), lambda step: (0, step)),
            pl.BlockSpec((group, rows, LANES), lambda step: (step, 0, 0)),
            full_spec(lows.shape),
        ]
        + [full_spec(block.shape) for block in blocks],
        out_specs=[
            pl.BlockSpec((group, rows, seq_total), lambda step: (step, 0, 0)),
            full_spec((rows, seq_total)),
            full_spec((seq_total, dims)),
        ],
        scratch_shapes=[pltpu.VMEM((rows, seq_total), jnp.float32)],
        compiler_params=pltpu.CompilerParams(vmem_limit_bytes=20 << 20),
        cost_estimate=pl.CostEstimate(
            flops=8 * rows * index_heads * seq_total * dims, bytes_accessed=0, transcendentals=0
        ),
        name="scores",
    )(index_query, scales, lows, *blocks)


def grads_kernel(peers, factor, own_ref, *refs):
    others = refs[: peers - 1]
    predicted_ref, active_ref, scale_ref, query_ref, keys_ref = refs[peers - 1 : peers + 4]
    grad_query_ref, grad_weight_ref, grad_key_ref, gap_ref, tall, weight_sum = refs[peers + 4 :]
    step = pl.program_id(0)
    heads, rows, seq_total = active_ref.shape
    dims = keys_ref.shape[1]
    slots = seq_total // LANES

    @pl.when(step == 0)
    def _():
        tall[...] = jnp.zeros_like(tall)
        weight_sum[...] = jnp.zeros_like(weight_sum)
        predicted = predicted_ref[...]
        seen = predicted >= 0.0
        mass = own_ref[...]
        for other in others:
            mass = mass + other[...].astype(jnp.float32)
        mass = jnp.where(seen, mass, 0.0)
        target = mass / jnp.sum(mass, axis=1, keepdims=True)
        gap_ref[...] = jnp.where(seen, predicted - target, 0.0)

    gap = gap_ref[...]
    lane = lax.broadcasted_iota(jnp.int32, (rows, LANES), 1)
    sums = weight_sum[...]
    slopes = []
    for head in range(heads):
        active = active_ref[head]
        product = active * gap
        partial = functools.reduce(
            jnp.add, [product[:, slot * LANES : (slot + 1) * LANES] for slot in range(slots)]
        )
        partial = jnp.sum(partial, axis=1, keepdims=True)
        sums = jnp.where(lane == step * heads + head, partial, sums)
        spread_gap = gap * jnp.concatenate([scale_ref[head]] * slots, axis=1)
        slope = jnp.where(active > 0.0, spread_gap, 0.0)
        slopes.append(slope if rows % 16 else slope.astype(jnp.bfloat16))
    weight_sum[...] = sums
    slopes = jnp.concatenate(slopes, axis=0).astype(jnp.bfloat16)
    grad_query = jnp.dot(slopes, keys_ref[...], preferred_element_type=jnp.float32)
    for head in range(heads):
        grad_query_ref[:, head * dims : (head + 1) * dims] = grad_query[head * rows : (head + 1) * rows]
    stacked = stack_heads(query_ref[...], heads, dims)
    tall[...] += lax.dot_general(
        stacked, slopes, (((0,), (0,)), ((), ())), preferred_element_type=jnp.float32
    )

    @pl.when(step == pl.num_programs(0) - 1)
    def _():
        grad_weight_ref[...] = sums[:, : grad_weight_ref.shape[1]] * factor
        seq = lax.axis_index("seq")
        for slot in range(slots):
            begin = pl.multiple_of(jnp.bitwise_xor(seq, slot) * LANES, LANES)
            part = jnp.transpose(tall[:, slot * LANES : (slot + 1) * LANES])
            grad_key_ref[pl.ds(begin, LANES), :] = part.astype(grad_key_ref.dtype)


def index_grads(own, others, predicted, active, scales, index_query, keys, factor):
    index_heads, rows, seq_total = active.shape
    dims = keys.shape[1]
    group = min(8, index_heads)
    peers = len(others) + 1
    flat = full_spec((rows, seq_total))
    return pl.pallas_call(
        functools.partial(grads_kernel, peers, factor),
        out_shape=(
            shape_of((rows, index_heads * dims), jnp.float32),
            shape_of((rows, index_heads), jnp.float32),
            shape_of((seq_total, dims), jnp.bfloat16),
        ),
        grid=(index_heads // group,),
        in_specs=[flat] * (peers + 1)
        + [
            pl.BlockSpec((group, rows, seq_total), lambda step: (step, 0, 0)),
            pl.BlockSpec((group, rows, LANES), lambda step: (step, 0, 0)),
            pl.BlockSpec((rows, group * dims), lambda step: (0, step)),
            full_spec(keys.shape),
        ],
        out_specs=[
            pl.BlockSpec((rows, group * dims), lambda step: (0, step)),
            full_spec((rows, index_heads)),
            full_spec((seq_total, dims)),
        ],
        scratch_shapes=[
            pltpu.VMEM((rows, seq_total), jnp.float32),
            pltpu.VMEM((dims, seq_total), jnp.float32),
            pltpu.VMEM((rows, LANES), jnp.float32),
        ],
        compiler_params=pltpu.CompilerParams(vmem_limit_bytes=20 << 20),
        cost_estimate=pl.CostEstimate(
            flops=8 * rows * index_heads * seq_total * dims, bytes_accessed=0, transcendentals=0
        ),
        name="grads",
    )(own, *others, predicted, active, scales, index_query, keys)


def per_device(lat_query, lat_keys, normalizer, lookback, index_query, index_keys, index_weight):
    seq_count = lax.axis_size("seq")
    peers = lax.axis_size("head")
    heads = lat_query.shape[1] // KDIM
    rows, index_heads = index_weight.shape
    dims = index_keys.shape[1]
    factor = dims ** (-0.5)

    def swap(value, bits):
        return lax.ppermute(value, "seq", [(place, place ^ bits) for place in range(seq_count)])

    mine = jnp.concatenate([lat_keys.T, index_keys], axis=0)
    blocks = [mine] + [swap(mine, bits) for bits in range(2, seq_count, 2)]
    blocks = [block for even in blocks for block in (even, swap(even, 1))]

    offsets, scales, lows = spread(normalizer, index_weight, lookback, heads, factor)
    active, predicted, keys = index_scores(index_query, scales, lows, blocks, dims)
    own, *sends = attention_mass(lat_query, offsets, blocks, rows, peers)
    others = [
        lax.ppermute(send, "head", [(place, (place + hop + 1) % peers) for place in range(peers)])
        for hop, send in enumerate(sends)
    ]
    grad_query, grad_weight, key_terms = index_grads(
        own, others, predicted, active, scales, index_query, keys, factor
    )
    arrived = lax.all_to_all(key_terms, ("seq", "head"), 0, 0, tiled=True)
    grad_key = jnp.sum(
        arrived.reshape(seq_count * peers, -1, dims).astype(jnp.float32), axis=0
    )
    return grad_query, grad_weight, grad_key


def solution(mesh):
    return jax.shard_map(
        per_device,
        mesh=mesh,
        in_specs=(
            P("seq", "head"),
            P("seq", None),
            P("seq", None),
            P("seq"),
            P(("seq", "head"), None),
            P("seq", None),
            P(("seq", "head"), None),
        ),
        out_specs=(P(("seq", "head"), None), P(("seq", "head"), None), P(("seq", "head"), None)),
        check_vma=False,
    )
```

time: 335 us -> 60.5 us (0.18)
  waiting for transfers between devices: 145 us -> 8.79 us
  local copies, waits for them, and re-layouts: 79.2 us -> 4.55 us
  other arithmetic: 43.5 us -> 1.6 us
  matrix products: 35.7 us -> 0 us
  Pallas kernels: 0 us -> 19.4 us
  between operations: 15.1 us -> 0.71 us
  starting transfers between devices: 0.3 us -> 10.6 us
    reduce_scatter x2 -> x0, waiting for transfers between devices: 134 us -> none  [the longest x1 134 us: per_device(): lax.psum_scatter(key_terms, ('seq', 'head'), scatter_dimension=0, tiled=T...]
    mul x12 -> x0, local copies, waits for them, and re-layouts: 56.8 us -> none  [the longest x6 23 us: scores(): active * flat_weight[:, None]]
    dot_general x10 -> x0, matrix products: 35.7 us -> none  [the longest x2 16.3 us: step(): lax.dot_general(flat_query, key_part, (((1,), (1,)), ((), ())), preferred...]
    reduce_sum x11 -> x1, other arithmetic: 31.8 us -> 0.65 us  [per_device(): jnp.sum(arrived.reshape(seq_count * peers, -1, dims).astype(jnp.float32),...]
    pallas_call x0 -> x4, Pallas kernels: none -> 19.4 us  [the longest x1 10.3 us: attention_mass(): pl.pallas_call(functools.partial(mass_kernel, slots, group), out_shape=ou...]
    all_to_all x0 -> x1, blocking collectives: none -> 14.5 us  [per_device(): arrived = lax.all_to_all(key_terms, ('seq', 'head'), 0, 0, tiled=True)]
    reshape x3 -> x0, local copies, waits for them, and re-layouts: 13.6 us -> none  [the longest x1 9.95 us: per_device(): flat_query = lat_query.reshape(local_rows * head_count, KDIM)]
    all_gather x1 -> x0, blocking collectives: 11.5 us -> none  [per_device(): indexed = lax.all_gather(index_keys, 'seq', axis=0, tiled=True)]
  transfers between devices with their start and end apart: 3 -> 10, of which waited for: 2 -> 5; matrix products, arithmetic and copies ran while one was open for 11% -> 0% of each run, Pallas kernels for 0% -> 7%
where the time goes in v1:
time: 60.5 us; the launch traced here: 60.2 us
  Pallas kernels  19.4 us (32%)
  blocking collectives  14.5 us (24%)
  starting transfers between devices  10.6 us (18%)
  waiting for transfers between devices  8.79 us (15%)
  local copies, waits for them, and re-layouts  4.55 us (8%)
  other arithmetic  1.6 us (3%)
  between operations  0.71 us (1%)
    all_to_all x1, blocking collectives, per_device(): arrived = lax.all_to_all(key_terms, ('seq', 'head'), 0, 0, tiled=True)  14.5 us
    pallas_call x1, Pallas kernels, attention_mass(): pl.pallas_call(functools.partial(mass_kernel, slots, group), out_shape=ou...  10.3 us
    ppermute x7, waiting for transfers between devices, swap(): lax.ppermute(value, 'seq', [(place, place ^ bits) for place in range(seq_...  8.05 us
    ppermute x3, starting transfers between devices, per_device(): lax.ppermute(send, 'head', [(place, (place + hop + 1) % peers) for place...  5.76 us
    pallas_call x1, Pallas kernels, index_grads(): pl.pallas_call(functools.partial(grads_kernel, peers, factor), out_shape=...  5.14 us
    ppermute x7, starting transfers between devices, swap(): lax.ppermute(value, 'seq', [(place, place ^ bits) for place in range(seq_...  4.87 us
    unnamed x10, local copies, waits for them, and re-layouts  4.55 us
    pallas_call x1, Pallas kernels, index_scores(): pl.pallas_call(functools.partial(score_kernel, slots), out_shape=(shape_o...  2.83 us
  transfers between devices with their start and end apart: 10, of which 5 were waited for; matrix products, arithmetic and copies ran while one was open for 0% of the time, Pallas kernels for 7%

profile of v1, /device:TPU:0, one launch (start us, length us, event | category | flops | bytes accessed | tf_op | source)
XLA Modules:
  0.0 60.2 jit_solution(11563334192628344426)
XLA Ops:
  0.6 0.9 %pad_maximum_fusion.refs_0_ = bf16[704,128]{1,0:T(8,128)(2,1)S(1)} fusion(bf16[128,128]{1,0:T(8,128)(2,1)} %param.12, bf16[576,128]{1,0:T(8,128)(2,1)} %bitcast.5), kind=kLoop, calls=%fused_computation.1 | loop fusion | flops 360448 | bytes 360448 | tf_op jit(solution)/shard_map/concatenate | solution.py:351
  1.6 4.0 %collective-permute-start.5 = (bf16[704,128]{1,0:T(8,128)(2,1)S(1)}, bf16[704,128]{1,0:T(8,128)(2,1)S(1)}, u32[]{:S(2)}, u32[]{:S(2)}) collective-permute-start(bf16[704,128]{1,0:T(8,128)(2,1)S(1)} %pad_maximum_fusion.refs_0_), channel_id=1, source_target_pairs={{0,24},{4,28},{8,16},{12,20},{16,8},{20,12},{24,0},{28,4},{1,25},{... | collective-permute-start | bytes 540680 | tf_op jit(solution)/shard_map/ppermute | solution.py:349
  5.6 0.5 collective-permute-start.3
  6.1 0.1 collective-permute-start.1
  6.2 0.0 collective-permute-start
  6.2 4.8 %collective-permute-done.5.refs_6_ = bf16[704,128]{1,0:T(8,128)(2,1)S(1)} collective-permute-done((bf16[704,128]{1,0:T(8,128)(2,1)S(1)}, bf16[704,128]{1,0:T(8,128)(2,1)S(1)}, u32[]{:S(2)}, u32[]{:S(2)}) %collective-permute-start.5) | collective-permute-done | bytes 180256 | tf_op jit(solution)/shard_map/ppermute | solution.py:349
  11.0 0.0 collective-permute-start.6
  11.0 3.0 %collective-permute-done.3.refs_4_ = bf16[704,128]{1,0:T(8,128)(2,1)S(1)} collective-permute-done((bf16[704,128]{1,0:T(8,128)(2,1)S(1)}, bf16[704,128]{1,0:T(8,128)(2,1)S(1)}, u32[]{:S(2)}, u32[]{:S(2)}) %collective-permute-start.3) | collective-permute-done | bytes 180256 | tf_op jit(solution)/shard_map/ppermute | solution.py:349
  14.0 0.0 collective-permute-start.4
  14.0 0.3 collective-permute-done.1.refs_2_
  14.3 0.2 collective-permute-start.2
  14.5 0.0 copy-start.1
  14.5 0.8 %copy-done.1 = f32[128,128]{1,0:T(8,128)S(1)} copy-done((f32[128,128]{1,0:T(8,128)S(1)}, f32[128,128]{1,0:T(8,128)}, u32[]{:S(2)}) %copy-start.1) | copy-done | bytes 65560
  15.3 0.0 copy-start.2
  15.3 0.7 %copy-done.2 = f32[32,64]{1,0:T(8,128)S(1)} copy-done((f32[32,64]{1,0:T(8,128)S(1)}, f32[32,64]{1,0:T(8,128)}, u32[]{:S(2)}) %copy-start.2) | copy-done | bytes 8216
  16.1 0.0 copy-start.3
  16.1 0.7 %copy-done.3 = s32[128]{0:T(128)S(1)} copy-done((s32[128]{0:T(128)S(1)}, s32[128]{0:T(128)}, u32[]{:S(2)}) %copy-start.3) | copy-done | bytes 536
  16.7 1.1 %spread.1 = (f32[32,128,128]{2,1,0:T(8,128)S(1)}, f32[64,32,128]{2,1,0:T(8,128)S(1)}, f32[32,128]{1,0:T(8,128)S(1)}) custom-call(f32[128,128]{1,0:T(8,128)S(1)} %copy-done.1, f32[32,64]{1,0:T(8,128)S(1)} %copy-done.2, s32[1,128]{1,0:T(1,128)S(1)} %bitcast.4), custom_call_target="tpu_custom_call" | custom-call | flops 4000000 | tf_op jit(solution)/shard_map/spread/pallas_call | solution.py:48
  17.8 0.0 collective-permute-done.refs_1_
  17.9 0.0 collective-permute-done.6.refs_7_
  17.9 0.0 collective-permute-done.4.refs_5_
  17.9 0.0 collective-permute-done.2.refs_3_
  17.9 0.0 copy-start.4
  17.9 2.3 %copy-done.4 = bf16[128,18432]{1,0:T(8,128)(2,1)S(1)} copy-done((bf16[128,18432]{1,0:T(8,128)(2,1)S(1)}, bf16[128,18432]{1,0:T(8,128)(2,1)}, u32[]{:S(2)}) %copy-start.4) | copy-done | bytes 4718616
  20.2 0.0 copy-start
  20.2 10.3 %mass.1 = (f32[32,1024]{1,0:T(8,128)S(1)}, bf16[32,1024]{1,0:T(8,128)(2,1)S(1)}, bf16[32,1024]{1,0:T(8,128)(2,1)S(1)}, bf16[32,1024]{1,0:T(8,128)(2,1)S(1)}) custom-call(bf16[128,18432]{1,0:T(8,128)(2,1)S(1)} %copy-done.4, f32[32,128,128]{2,1,0:T(8,128)S(1)} %get-tuple-element.16.off_ref, bf16[704,128]{1,0:T(8,128)(2,1)S(1)} %pad_maximum_fusion.refs_0_, ...), custom_call_target="tpu_custom_call" | custom-call | flops 4831838208 | tf_op jit(solution)/shard_map/mass/pallas_call | solution.py:126
  30.6 1.8 %collective-permute-start.7 = (bf16[32,1024]{1,0:T(8,128)(2,1)S(1)}, bf16[32,1024]{1,0:T(8,128)(2,1)S(1)}, u32[]{:S(2)}, u32[]{:S(2)}) collective-permute-start(bf16[32,1024]{1,0:T(8,128)(2,1)S(1)} %get-tuple-element.18), channel_id=1, source_target_pairs={{0,1},{1,2},{2,3},{3,0},{4,5},{5,6},{6,7},{7,4},{8,9},{9,10},{10,1... | collective-permute-start | bytes 196616 | tf_op jit(solution)/shard_map/ppermute | solution.py:359
  32.4 2.6 %collective-permute-start.8 = (bf16[32,1024]{1,0:T(8,128)(2,1)S(1)}, bf16[32,1024]{1,0:T(8,128)(2,1)S(1)}, u32[]{:S(2)}, u32[]{:S(2)}) collective-permute-start(bf16[32,1024]{1,0:T(8,128)(2,1)S(1)} %get-tuple-element.19), channel_id=1, source_target_pairs={{0,2},{1,3},{2,0},{3,1},{4,6},{5,7},{6,4},{7,5},{8,10},{9,11},{10,... | collective-permute-start | bytes 196616 | tf_op jit(solution)/shard_map/ppermute | solution.py:359
  35.0 1.3 %collective-permute-start.9 = (bf16[32,1024]{1,0:T(8,128)(2,1)S(1)}, bf16[32,1024]{1,0:T(8,128)(2,1)S(1)}, u32[]{:S(2)}, u32[]{:S(2)}) collective-permute-start(bf16[32,1024]{1,0:T(8,128)(2,1)S(1)} %get-tuple-element.20), channel_id=1, source_target_pairs={{0,3},{1,0},{2,1},{3,2},{4,7},{5,4},{6,5},{7,6},{8,11},{9,8},{10,9... | collective-permute-start | bytes 196616 | tf_op jit(solution)/shard_map/ppermute | solution.py:359
  36.3 0.0 copy-done
  36.3 2.8 %scores.1 = (f32[64,32,1024]{2,1,0:T(8,128)S(1)}, f32[32,1024]{1,0:T(8,128)S(1)}, bf16[1024,128]{1,0:T(8,128)(2,1)S(1)}) custom-call(bf16[32,8192]{1,0:T(8,128)(2,1)S(1)} %copy-done, f32[64,32,128]{2,1,0:T(8,128)S(1)} %get-tuple-element.21.scale_ref.refs_5_, f32[32,128]{1,0:T(8,128)S(1)} %get-tuple-element.22.low_ref, ...), custom_call_target="tpu_custom_call" | custom-call | flops 2147483648 | tf_op jit(solution)/shard_map/scores/pallas_call | solution.py:216
  39.2 0.0 collective-permute-done.7.refs_0_
  39.2 0.5 collective-permute-done.8.refs_1_
  39.7 0.2 collective-permute-done.9.refs_2_
  39.9 5.1 %grads.1 = (f32[32,8192]{1,0:T(8,128)}, f32[32,64]{1,0:T(8,128)}, bf16[1024,128]{1,0:T(8,128)(2,1)S(1)}) custom-call(f32[32,1024]{1,0:T(8,128)S(1)} %get-tuple-element.17.own_ref, bf16[32,1024]{1,0:T(8,128)(2,1)S(1)} %collective-permute-done.7.refs_0_, bf16[32,1024]{1,0:T(8,128)(2,1)S(1)} %collective-permute-done.8.refs_1_, ...), custom_call_target="tpu_custom_call" | custom-call | flops 2147483648 | tf_op jit(solution)/shard_map/grads/pallas_call | solution.py:307
  45.0 14.5 %all_to_all.9 = bf16[32,32,128]{2,1,0:T(8,128)(2,1)S(1)} all-to-all(bf16[32,32,128]{2,1,0:T(8,128)(2,1)S(1)} %bitcast.3), channel_id=1, replica_groups=mesh['seq'=8,'head'=4] {'seq','head'}, dimensions={0} | all-to-all | bytes 524288 | tf_op jit(solution)/shard_map/all_to_all | solution.py:365
  59.5 0.7 %convert_reduce_fusion = f32[32,128]{1,0:T(8,128)} fusion(bf16[32,32,128]{2,1,0:T(8,128)(2,1)S(1)} %all_to_all.9), kind=kLoop, calls=%fused_computation | loop fusion | flops 258048 | bytes 278528 | tf_op jit(solution)/shard_map/reduce_sum | solution.py:366
Async XLA Ops:
  1.6 9.4 %collective-permute-start.5 = (bf16[704,128]{1,0:T(8,128)(2,1)S(1)}, bf16[704,128]{1,0:T(8,128)(2,1)S(1)}, u32[]{:S(2)}, u32[]{:S(2)}) collective-permute-start(bf16[704,128]{1,0:T(8,128)(2,1)S(1)} %pad_maximum_fusion.refs_0_), channel_id=1, source_target_pairs={{0,24},{4,28},{8,16},{12,20},{16,8},{20,12},{24,0},{28,4},{1,25},{... | collective-permute-start | bytes 540680 | tf_op jit(solution)/shard_map/ppermute | solution.py:349
  5.6 8.4 %collective-permute-start.3 = (bf16[704,128]{1,0:T(8,128)(2,1)S(1)}, bf16[704,128]{1,0:T(8,128)(2,1)S(1)}, u32[]{:S(2)}, u32[]{:S(2)}) collective-permute-start(bf16[704,128]{1,0:T(8,128)(2,1)S(1)} %pad_maximum_fusion.refs_0_), channel_id=1, source_target_pairs={{0,16},{4,20},{8,24},{12,28},{16,0},{20,4},{24,8},{28,12},{1,17},{... | collective-permute-start | bytes 540680 | tf_op jit(solution)/shard_map/ppermute | solution.py:349
  6.1 8.2 %collective-permute-start.1 = (bf16[704,128]{1,0:T(8,128)(2,1)S(1)}, bf16[704,128]{1,0:T(8,128)(2,1)S(1)}, u32[]{:S(2)}, u32[]{:S(2)}) collective-permute-start(bf16[704,128]{1,0:T(8,128)(2,1)S(1)} %pad_maximum_fusion.refs_0_), channel_id=1, source_target_pairs={{0,8},{4,12},{8,0},{12,4},{16,24},{20,28},{24,16},{28,20},{1,9},{5... | collective-permute-start | bytes 540680 | tf_op jit(solution)/shard_map/ppermute | solution.py:349
  6.2 11.6 %collective-permute-start = (bf16[704,128]{1,0:T(8,128)(2,1)S(1)}, bf16[704,128]{1,0:T(8,128)(2,1)S(1)}, u32[]{:S(2)}, u32[]{:S(2)}) collective-permute-start(bf16[704,128]{1,0:T(8,128)(2,1)S(1)} %pad_maximum_fusion.refs_0_), channel_id=1, source_target_pairs={{0,4},{4,0},{8,12},{12,8},{16,20},{20,16},{24,28},{28,24},{1,5},{5... | collective-permute-start | bytes 540680 | tf_op jit(solution)/shard_map/ppermute | solution.py:349
  11.0 6.9 %collective-permute-start.6 = (bf16[704,128]{1,0:T(8,128)(2,1)S(1)}, bf16[704,128]{1,0:T(8,128)(2,1)S(1)}, u32[]{:S(2)}, u32[]{:S(2)}) collective-permute-start(bf16[704,128]{1,0:T(8,128)(2,1)S(1)} %collective-permute-done.5.refs_6_), channel_id=1, source_target_pairs={{0,4},{4,0},{8,12},{12,8},{16,20},{20,16},{24,28},{28,24},{1,5},{5... | collective-permute-start | bytes 540680 | tf_op jit(solution)/shard_map/ppermute | solution.py:349
  14.0 3.9 %collective-permute-start.4 = (bf16[704,128]{1,0:T(8,128)(2,1)S(1)}, bf16[704,128]{1,0:T(8,128)(2,1)S(1)}, u32[]{:S(2)}, u32[]{:S(2)}) collective-permute-start(bf16[704,128]{1,0:T(8,128)(2,1)S(1)} %collective-permute-done.3.refs_4_), channel_id=1, source_target_pairs={{0,4},{4,0},{8,12},{12,8},{16,20},{20,16},{24,28},{28,24},{1,5},{5... | collective-permute-start | bytes 540680 | tf_op jit(solution)/shard_map/ppermute | solution.py:349
  14.3 3.6 %collective-permute-start.2 = (bf16[704,128]{1,0:T(8,128)(2,1)S(1)}, bf16[704,128]{1,0:T(8,128)(2,1)S(1)}, u32[]{:S(2)}, u32[]{:S(2)}) collective-permute-start(bf16[704,128]{1,0:T(8,128)(2,1)S(1)} %collective-permute-done.1.refs_2_), channel_id=1, source_target_pairs={{0,4},{4,0},{8,12},{12,8},{16,20},{20,16},{24,28},{28,24},{1,5},{5... | collective-permute-start | bytes 540680 | tf_op jit(solution)/shard_map/ppermute | solution.py:349
  14.5 0.8 %copy-start.1 = (f32[128,128]{1,0:T(8,128)S(1)}, f32[128,128]{1,0:T(8,128)}, u32[]{:S(2)}) copy-start(f32[128,128]{1,0:T(8,128)} %norm_ref.1) | copy-start | bytes 196612
  15.3 0.7 %copy-start.2 = (f32[32,64]{1,0:T(8,128)S(1)}, f32[32,64]{1,0:T(8,128)}, u32[]{:S(2)}) copy-start(f32[32,64]{1,0:T(8,128)} %weight_ref.1) | copy-start | bytes 24580
  16.1 0.7 %copy-start.3 = (s32[128]{0:T(128)S(1)}, s32[128]{0:T(128)}, u32[]{:S(2)}) copy-start(s32[128]{0:T(128)} %param.10) | copy-start | bytes 1540
  17.9 2.3 %copy-start.4 = (bf16[128,18432]{1,0:T(8,128)(2,1)S(1)}, bf16[128,18432]{1,0:T(8,128)(2,1)}, u32[]{:S(2)}) copy-start(bf16[128,18432]{1,0:T(8,128)(2,1)} %query_ref.2) | copy-start | bytes 14155780
  20.2 16.1 %copy-start = (bf16[32,8192]{1,0:T(8,128)(2,1)S(1)}, bf16[32,8192]{1,0:T(8,128)(2,1)}, u32[]{:S(2)}) copy-start(bf16[32,8192]{1,0:T(8,128)(2,1)} %refs_6_.1) | copy-start | bytes 1572868
  30.6 8.6 %collective-permute-start.7 = (bf16[32,1024]{1,0:T(8,128)(2,1)S(1)}, bf16[32,1024]{1,0:T(8,128)(2,1)S(1)}, u32[]{:S(2)}, u32[]{:S(2)}) collective-permute-start(bf16[32,1024]{1,0:T(8,128)(2,1)S(1)} %get-tuple-element.18), channel_id=1, source_target_pairs={{0,1},{1,2},{2,3},{3,0},{4,5},{5,6},{6,7},{7,4},{8,9},{9,10},{10,1... | collective-permute-start | bytes 196616 | tf_op jit(solution)/shard_map/ppermute | solution.py:359
  32.4 7.3 %collective-permute-start.8 = (bf16[32,1024]{1,0:T(8,128)(2,1)S(1)}, bf16[32,1024]{1,0:T(8,128)(2,1)S(1)}, u32[]{:S(2)}, u32[]{:S(2)}) collective-permute-start(bf16[32,1024]{1,0:T(8,128)(2,1)S(1)} %get-tuple-element.19), channel_id=1, source_target_pairs={{0,2},{1,3},{2,0},{3,1},{4,6},{5,7},{6,4},{7,5},{8,10},{9,11},{10,... | collective-permute-start | bytes 196616 | tf_op jit(solution)/shard_map/ppermute | solution.py:359
  35.0 4.9 %collective-permute-start.9 = (bf16[32,1024]{1,0:T(8,128)(2,1)S(1)}, bf16[32,1024]{1,0:T(8,128)(2,1)S(1)}, u32[]{:S(2)}, u32[]{:S(2)}) collective-permute-start(bf16[32,1024]{1,0:T(8,128)(2,1)S(1)} %get-tuple-element.20), channel_id=1, source_target_pairs={{0,3},{1,0},{2,1},{3,2},{4,7},{5,4},{6,5},{7,6},{8,11},{9,8},{10,9... | collective-permute-start | bytes 196616 | tf_op jit(solution)/shard_map/ppermute | solution.py:359
